TPU v7x, 32 devices: a whole 2x2x4 slice. The times are simulated.
32 devices in a mesh: row: 4 (over z), col: 8 (over y, x, core).
Axes of the slice: x: 2, y: 2, z: 4, core: 2. Of those that a mesh axis runs over, the one named last changes fastest.
Arguments:
- grad: float32 [8192, 14336], P(('row', 'col')), may hold values from -30 to 30
- momentum: float32 [8192, 14336], P(('row', 'col')), may hold values from -6 to 6
- weight: float32 [8192, 14336], P(('row', 'col')), may hold values from -0.75 to 0.75
Outputs:
- new_weight: float32 [8192, 14336], P('row', 'col')
- new_momentum: float32 [8192, 14336], P('row', 'col')
All inputs are finite; a program needn't handle non-finite values.
Results may differ from a plain program's by a relative error of at most 0.00002.
Values sent between devices are 32-bit elements; how exact they have to be, the bound alone decides.
A program may use at most 192 MiB of HBM per device.

v0:
```python
import math

import jax
import jax.numpy as jnp
from jax import lax
from jax.sharding import PartitionSpec as P

D = 8192
FF = 14336


def update_state(total, grad, momentum, weight):
    limit = jnp.float32(math.sqrt(D * FF))
    factor = jnp.minimum(jnp.float32(1.0), limit / (jnp.sqrt(total) + jnp.float32(1e-06)))
    new_momentum = jnp.float32(0.9) * momentum + factor * grad
    new_weight = weight - jnp.float32(0.1) * new_momentum
    return (new_weight, new_momentum)


def body(grad, momentum, weight):
    total = lax.psum(jnp.sum(grad * grad), ("row", "col"))
    local_weight, local_momentum = update_state(total, grad, momentum, weight)
    new_weight, new_momentum = (
        lax.all_to_all(local_weight, "col", split_axis=1, concat_axis=0, tiled=True),
        lax.all_to_all(local_momentum, "col", split_axis=1, concat_axis=0, tiled=True),
    )
    return (new_weight, new_momentum)


def solution(mesh):
    in_specs = (P(("row", "col"), None), P(("row", "col"), None), P(("row", "col"), None))
    out_specs = (P("row", "col"), P("row", "col"))
    return jax.shard_map(body, mesh=mesh, in_specs=in_specs, out_specs=out_specs, check_vma=False)
```

profile of v0, /device:TPU:0, one launch (start us, length us, event | category | flops | bytes accessed | tf_op | source)
XLA Modules:
  0.0 447.5 jit_solution(14981939035309159026)
XLA Ops:
  0.6 9.6 %multiply_reduce_fusion = f32[]{:T(128)} fusion(f32[256,14336]{1,0:T(8,128)} %param.3), kind=kLoop, calls=%fused_computation.4 | loop fusion | flops 7340031 | bytes 14680068 | tf_op jit(solution)/shard_map/reduce_sum | solution.py:21
  10.2 42.2 %psum.7 = f32[]{:T(128)} all-reduce(f32[]{:T(128)} %multiply_reduce_fusion), channel_id=1, replica_groups=mesh['row'=4,'col'=8] {'row','col'}, use_global_device_ids=true, to_apply=%region_1.0 | all-reduce | flops 1 | bytes 8 | tf_op jit(solution)/shard_map/psum | solution.py:21
  53.1 25.5 %multiply_subtract_fusion = (f32[256,14336]{1,0:T(8,128)}, f32[256,14336]{1,0:T(8,128)}) fusion(f32[256,14336]{1,0:T(8,128)} %param.5, f32[256,14336]{1,0:T(8,128)} %param.3, f32[]{:T(128)S(6)} %min_shard_map.3, f32[256,14336]{1,0:T(8,128)} %param.4), kind=kLoop, calls=%fused_computation.2 | loop fusion | flops 18350080 | bytes 73400320 | tf_op jit(solution)/shard_map/sub | solution.py:16
  78.6 11.8 %copy.11 = f32[32,8,8,1792]{3,2,0,1:T(8,128)} copy(f32[32,8,8,1792]{3,2,1,0:T(8,128)} %bitcast.17) | data formatting | bytes 29360128 | tf_op jit(solution)/shard_map/all_to_all | solution.py:25
  90.3 5.5 %all-to-all-start.1 = ((f32[256,8,1792]{2,0,1:T(8,128)}), f32[256,8,1792]{2,0,1:T(8,128)}, u32[]{:S(2)}, u32[]{:S(2)}) async-start(f32[256,8,1792]{2,0,1:T(8,128)} %bitcast.15), calls=%async_computation.1 | async-start | bytes 29360128 | tf_op jit(solution)/shard_map/all_to_all | solution.py:25
  95.9 12.0 %copy.12 = f32[32,8,8,1792]{3,2,0,1:T(8,128)} copy(f32[32,8,8,1792]{3,2,1,0:T(8,128)} %bitcast.16) | data formatting | bytes 29360128 | tf_op jit(solution)/shard_map/all_to_all | solution.py:24
  107.9 149.4 %all-to-all-done.1 = f32[256,8,1792]{2,0,1:T(8,128)} async-done(((f32[256,8,1792]{2,0,1:T(8,128)}), f32[256,8,1792]{2,0,1:T(8,128)}, u32[]{:S(2)}, u32[]{:S(2)}) %all-to-all-start.1) | async-done | bytes 14680096 | tf_op jit(solution)/shard_map/all_to_all | solution.py:25
  257.3 5.5 %all-to-all-start = ((f32[256,8,1792]{2,0,1:T(8,128)}), f32[256,8,1792]{2,0,1:T(8,128)}, u32[]{:S(2)}, u32[]{:S(2)}) async-start(f32[256,8,1792]{2,0,1:T(8,128)} %bitcast.14), calls=%async_computation | async-start | bytes 29360128 | tf_op jit(solution)/shard_map/all_to_all | solution.py:24
  262.9 161.5 %all-to-all-done = f32[256,8,1792]{2,0,1:T(8,128)} async-done(((f32[256,8,1792]{2,0,1:T(8,128)}), f32[256,8,1792]{2,0,1:T(8,128)}, u32[]{:S(2)}, u32[]{:S(2)}) %all-to-all-start) | async-done | bytes 14680096 | tf_op jit(solution)/shard_map/all_to_all | solution.py:24
  424.3 11.6 %copy.15 = f32[2048,1792]{1,0:T(8,128)} copy(f32[2048,1792]{1,0:T(8,128)} %bitcast.1) | data formatting | bytes 29360128
  435.9 11.6 %copy.16 = f32[2048,1792]{1,0:T(8,128)} copy(f32[2048,1792]{1,0:T(8,128)} %bitcast.3) | data formatting | bytes 29360128
Async XLA Ops:
  90.3 167.0 %all-to-all-start.1 = ((f32[256,8,1792]{2,0,1:T(8,128)}), f32[256,8,1792]{2,0,1:T(8,128)}, u32[]{:S(2)}, u32[]{:S(2)}) async-start(f32[256,8,1792]{2,0,1:T(8,128)} %bitcast.15), calls=%async_computation.1 | async-start | bytes 29360128 | tf_op jit(solution)/shard_map/all_to_all | solution.py:25
  257.3 167.0 %all-to-all-start = ((f32[256,8,1792]{2,0,1:T(8,128)}), f32[256,8,1792]{2,0,1:T(8,128)}, u32[]{:S(2)}, u32[]{:S(2)}) async-start(f32[256,8,1792]{2,0,1:T(8,128)} %bitcast.14), calls=%async_computation | async-start | bytes 29360128 | tf_op jit(solution)/shard_map/all_to_all | solution.py:24
where the time goes:
time: 448 us; the launch traced here: 447 us
  waiting for transfers between devices  311 us (69%)
  local copies, waits for them, and re-layouts  47 us (10%)
  blocking collectives  42.2 us (9%)
  other arithmetic  35 us (8%)
  starting transfers between devices  11.1 us (2%)
    all_to_all x1, waiting for transfers between devices, body(): lax.all_to_all(local_weight, 'col', split_axis=1, concat_axis=0, tiled=True)  161 us
    all_to_all x1, waiting for transfers between devices, body(): lax.all_to_all(local_momentum, 'col', split_axis=1, concat_axis=0, tiled=...  149 us
    psum x1, blocking collectives, body(): total = lax.psum(jnp.sum(grad * grad), ('row', 'col'))  42.2 us
    sub x1, other arithmetic, update_state(): new_weight = weight - jnp.float32(0.1) * new_momentum  25.5 us
    unnamed x2, local copies, waits for them, and re-layouts  23.2 us
    all_to_all x1, local copies, waits for them, and re-layouts, body(): lax.all_to_all(local_weight, 'col', split_axis=1, concat_axis=0, tiled=True)  12 us
    all_to_all x1, local copies, waits for them, and re-layouts, body(): lax.all_to_all(local_momentum, 'col', split_axis=1, concat_axis=0, tiled=...  11.8 us
    reduce_sum x1, other arithmetic, body(): total = lax.psum(jnp.sum(grad * grad), ('row', 'col'))  9.55 us
  transfers between devices with their start and end apart: 2, of which 2 were waited for; matrix products, arithmetic and copies ran while one was open for 3% of the time, Pallas kernels for 0%

commit v1 on v0

v1 whole, which is shorter than its diff:
```python
import functools
import math

import jax
import jax.numpy as jnp
from jax import lax
from jax.experimental import pallas as pl
from jax.experimental.pallas import tpu as pltpu
from jax.sharding import PartitionSpec as P

F32 = jnp.float32
MESH = pl.DeviceIdType.MESH
MIB = 1 << 20


def partner(me, k, n):
    if n & (n - 1):
        return lax.rem(me + k, n)
    index, bit = 0, 1
    while bit < n:
        own = lax.rem(me // bit, 2)
        index = index + (1 - own if k & bit else own) * bit
        bit *= 2
    return index


def source(me, k, n):
    return lax.rem(me + n - k, n) if n & (n - 1) else partner(me, k, n)


def exchange(
    n, nr, limit, head, step,
    g_ref, m_ref, w_ref, w_out, nm_out,
    gbuf, mbuf, part, col_parts, row_parts,
    g_sem, m_sem, own_sem, w_send, w_recv, nm_send, nm_recv, cs_sem, cr_sem, rs_sem, rr_sem,
):
    rows, width = g_ref.shape
    cols = width // n
    me, me_row = lax.axis_index("col"), lax.axis_index("row")
    chunks = rows // step

    def window(index):
        return pl.ds(pl.multiple_of(index * cols, 128), cols)

    def landing(index, start, size):
        return pl.ds(pl.multiple_of(index * rows + start, 8), size)

    def piece(src, dst, to, frm, start, size, send, recv, k, part_index):
        out = pltpu.make_async_remote_copy(
            src_ref=src.at[pl.ds(start, size), window(to)],
            dst_ref=dst.at[landing(me, start, size), :],
            send_sem=send.at[k, part_index], recv_sem=recv.at[k, part_index],
            device_id={"col": to}, device_id_type=MESH,
        )
        arriving = pltpu.make_async_remote_copy(
            src_ref=src.at[pl.ds(start, size), window(to)],
            dst_ref=dst.at[landing(frm, start, size), :],
            send_sem=send.at[k, part_index], recv_sem=recv.at[k, part_index],
            device_id={"col": to}, device_id_type=MESH,
        )
        return out, arriving

    peers = {k: (partner(me, k, n), source(me, k, n)) for k in range(1, n)}
    near = [k for k in peers if k >> 1 == 0]
    direct = [k for k in peers if k >> 1 and not (k >> 1) & ((k >> 1) - 1)]
    routed = [k for k in peers if k not in near and k not in direct]

    g_loads = [
        pltpu.make_async_copy(g_ref.at[pl.ds(c * step, step)], gbuf.at[pl.ds(c * step, step)], g_sem.at[c])
        for c in range(chunks)
    ]
    for load in g_loads:
        load.start()

    def m_load(c):
        return pltpu.make_async_copy(m_ref.at[pl.ds(c * step, step)], mbuf.at[c % 2], m_sem.at[c % 2])

    barrier = pltpu.get_barrier_semaphore()
    for k in peers:
        pl.semaphore_signal(barrier, inc=1, device_id={"col": peers[k][0]}, device_id_type=MESH)
    for k in range(1, nr):
        pl.semaphore_signal(barrier, inc=1, device_id={"row": partner(me_row, k, nr)}, device_id_type=MESH)
    pl.semaphore_wait(barrier, n - 1 + nr - 1)

    w_first = {k: piece(w_ref, w_out, *peers[k], 0, head, w_send, w_recv, k, 0) for k in peers}
    w_rest = {k: piece(w_ref, w_out, *peers[k], head, rows - head, w_send, w_recv, k, 1) for k in peers}
    nm_all = {k: piece(gbuf, nm_out, *peers[k], 0, rows, nm_send, nm_recv, k, 0) for k in peers}

    for k in direct:
        w_first[k][0].start()

    total = jnp.zeros((8, cols), F32)
    for c in range(chunks):
        g_loads[c].wait()

        def add(r, total, c=c):
            start = pl.multiple_of(c * step + r * 8, 8)
            for p in range(n):
                x = gbuf[pl.ds(start, 8), pl.ds(p * cols, cols)]
                total = total + x * x
            return total

        total = lax.fori_loop(0, step // 8, add, total)
    tile = total[:, 0:128]
    for p in range(1, cols // 128):
        tile = tile + total[:, p * 128 : (p + 1) * 128]
    part[...] = tile
    col_parts[me] = tile

    for c in range(2):
        m_load(c).start()
    own_w = pltpu.make_async_copy(w_ref.at[:, window(me)], w_out.at[landing(me, 0, rows), :], own_sem.at[0])
    own_w.start()

    def col_share(k, slot):
        return pltpu.make_async_remote_copy(
            src_ref=part, dst_ref=col_parts.at[slot], send_sem=cs_sem.at[k], recv_sem=cr_sem.at[k],
            device_id={"col": peers[k][0]}, device_id_type=MESH,
        )

    for k in peers:
        col_share(k, me).start()

    for k in direct:
        w_rest[k][0].start()
    for k in routed:
        w_rest[k][0].start()
    for k in routed:
        w_first[k][0].start()
    for k in near:
        w_first[k][0].start()
        w_rest[k][0].start()

    for k in peers:
        col_share(k, peers[k][1]).wait_recv()

    def row_share(k, slot):
        return pltpu.make_async_remote_copy(
            src_ref=col_parts, dst_ref=row_parts.at[slot], send_sem=rs_sem.at[k], recv_sem=rr_sem.at[k],
            device_id={"row": partner(me_row, k, nr)}, device_id_type=MESH,
        )

    for k in range(1, nr):
        row_share(k, me_row).start()
    row_parts[me_row] = col_parts[...]
    for k in range(1, nr):
        row_share(k, source(me_row, k, nr)).wait_recv()

    square = jnp.sum(row_parts[...].reshape(nr * n * 8, 128), keepdims=True)
    factor = jnp.minimum(F32(1.0), F32(limit) / (jnp.sqrt(square) + F32(1e-06)))
    factor = jnp.broadcast_to(factor, (8, cols))

    for c in range(chunks):
        m_load(c).wait()

        def update(r, carry, c=c):
            start = pl.multiple_of(c * step + r * 8, 8)
            for p in range(n):
                span = pl.ds(p * cols, cols)
                m = mbuf[c % 2, pl.ds(pl.multiple_of(r * 8, 8), 8), span]
                gbuf[pl.ds(start, 8), span] = F32(0.9) * m + factor * gbuf[pl.ds(start, 8), span]
            return carry

        lax.fori_loop(0, step // 8, update, 0)
        if c + 2 < chunks:
            m_load(c + 2).start()

    for k in routed:
        w_rest[k][0].wait_send()
    for k in direct + routed + near:
        nm_all[k][0].start()
    own_nm = pltpu.make_async_copy(gbuf.at[:, window(me)], nm_out.at[landing(me, 0, rows), :], own_sem.at[1])
    own_nm.start()

    for k in peers:
        w_first[k][0].wait_send()
        if k not in routed:
            w_rest[k][0].wait_send()
        col_share(k, me).wait_send()
    for k in range(1, nr):
        row_share(k, me_row).wait_send()
    own_w.wait()
    own_nm.wait()
    for k in peers:
        w_first[k][1].wait_recv()
        w_rest[k][1].wait_recv()
    for k in peers:
        nm_all[k][0].wait_send()
        nm_all[k][1].wait_recv()


def finish(block, w_ref, nm_ref, nw_out, nm_out, buf, nw_sem, nm_sem):
    rows = w_ref.shape[0]
    blocks = rows // block
    whole = pltpu.make_async_copy(nm_ref, nm_out, nm_sem)

    def write(b):
        return pltpu.make_async_copy(buf.at[b], nw_out.at[pl.ds(b * block, block)], nw_sem.at[b])

    for b in range(blocks):
        if b == 1:
            whole.start()

        def step(r, carry, b=b):
            start = pl.multiple_of(b * block + r * 8, 8)
            buf[b, pl.ds(pl.multiple_of(r * 8, 8), 8)] = w_ref[pl.ds(start, 8)] - F32(0.1) * nm_ref[pl.ds(start, 8)]
            return carry

        lax.fori_loop(0, block // 8, step, 0)
        write(b).start()
    whole.wait()
    for b in range(blocks):
        write(b).wait()


def body(n, nr, grad, momentum, weight):
    rows, width = grad.shape
    cols = width // n
    limit = math.sqrt(rows * n * nr * width)
    head = max(8, rows // 64 * 8)
    step = max(8, rows // 64 * 8)
    dma = pltpu.SemaphoreType.DMA
    anywhere, vmem = pl.BlockSpec(memory_space=pl.ANY), pl.BlockSpec(memory_space=pltpu.VMEM)
    local = rows * width * 4
    w_new, nm_new = pl.pallas_call(
        functools.partial(exchange, n, nr, limit, head, step),
        out_shape=(pltpu.VMEM((n * rows, cols), F32),) * 2,
        in_specs=[anywhere] * 3,
        out_specs=(vmem,) * 2,
        scratch_shapes=[
            pltpu.VMEM((rows, width), F32),
            pltpu.VMEM((2, step, width), F32),
            pltpu.VMEM((8, 128), F32),
            pltpu.VMEM((n, 8, 128), F32),
            pltpu.VMEM((nr, n, 8, 128), F32),
            dma((rows // step,)), dma((2,)), dma((2,)),
            dma((n, 2)), dma((n, 2)), dma((n, 1)), dma((n, 1)),
            dma((n,)), dma((n,)), dma((nr,)), dma((nr,)),
        ],
        compiler_params=pltpu.CompilerParams(
            collective_id=0, has_side_effects=True,
            vmem_limit_bytes=local + 2 * step * width * 4 + 2 * MIB,
        ),
        name="exchange",
    )(grad, momentum, weight)
    block = n * rows // 16
    return pl.pallas_call(
        functools.partial(finish, block),
        out_shape=(jax.ShapeDtypeStruct((n * rows, cols), F32),) * 2,
        in_specs=[vmem] * 2,
        out_specs=(anywhere,) * 2,
        scratch_shapes=[pltpu.VMEM((16, block, cols), F32), dma((16,)), dma],
        compiler_params=pltpu.CompilerParams(vmem_limit_bytes=local + 2 * MIB),
        name="finish",
    )(w_new, nm_new)


def solution(mesh):
    n, nr = mesh.shape["col"], mesh.shape["row"]
    spread = P(("row", "col"), None)
    return jax.shard_map(
        functools.partial(body, n, nr),
        mesh=mesh,
        in_specs=(spread,) * 3,
        out_specs=(P("row", "col"),) * 2,
        check_vma=False,
    )
```

time: 448 us -> 334 us (0.75)
  Pallas kernels: 0 us -> 333 us
  waiting for transfers between devices: 311 us -> 0 us
  local copies, waits for them, and re-layouts: 47 us -> 0 us
  blocking collectives: 42.2 us -> 0 us
  other arithmetic: 35 us -> 0 us
  starting transfers between devices: 11.1 us -> 0 us
    pallas_call x0 -> x2, Pallas kernels: none -> 333 us  [the longest x1 323 us: body(): pl.pallas_call(functools.partial(exchange, n, nr, limit, head, step), out...]
    all_to_all x2 -> x0, waiting for transfers between devices: 311 us -> none  [the longest x1 161 us: body(): lax.all_to_all(local_weight, 'col', split_axis=1, concat_axis=0, tiled=True)]
    psum x1 -> x0, blocking collectives: 42.2 us -> none  [body(): total = lax.psum(jnp.sum(grad * grad), ('row', 'col'))]
    sub x1 -> x0, other arithmetic: 25.5 us -> none  [update_state(): new_weight = weight - jnp.float32(0.1) * new_momentum]
    all_to_all x2 -> x0, local copies, waits for them, and re-layouts: 23.8 us -> none  [the longest x1 12 us: body(): lax.all_to_all(local_weight, 'col', split_axis=1, concat_axis=0, tiled=True)]
    unnamed x2 -> x0, local copies, waits for them, and re-layouts: 23.2 us -> none
    all_to_all x2 -> x0, starting transfers between devices: 11.1 us -> none  [the longest x1 5.55 us: body(): lax.all_to_all(local_momentum, 'col', split_axis=1, concat_axis=0, tiled=...]
    reduce_sum x1 -> x0, other arithmetic: 9.55 us -> none  [body(): total = lax.psum(jnp.sum(grad * grad), ('row', 'col'))]
  transfers between devices with their start and end apart: 2 -> 0, of which waited for: 2 -> 0; matrix products, arithmetic and copies ran while one was open for 3% -> 0% of each run, Pallas kernels for 0% -> 0%
where the time goes in v1:
time: 334 us
  Pallas kernels  333 us (100%)
    pallas_call x1, Pallas kernels, body(): pl.pallas_call(functools.partial(exchange, n, nr, limit, head, step), out...  323 us
    pallas_call x1, Pallas kernels, body(): pl.pallas_call(functools.partial(finish, block), out_shape=(jax.ShapeDtyp...  10.2 us

profile of v1, /device:TPU:0, one launch (start us, length us, event | category | flops | bytes accessed | tf_op | source)
XLA Modules:
  0.0 333.7 jit_solution(6586827059742956338)
XLA Ops:
  0.6 322.8 %exchange.1 = (f32[2048,1792]{1,0:T(8,128)S(1)}, f32[2048,1792]{1,0:T(8,128)S(1)}) custom-call(f32[256,14336]{1,0:T(8,128)} %g_ref.1, f32[256,14336]{1,0:T(8,128)} %m_ref.1, f32[256,14336]{1,0:T(8,128)} %w_ref.1), custom_call_target="tpu_custom_call" | custom-call | tf_op jit(solution)/shard_map/exchange/pallas_call | solution.py:225
  323.5 10.2 %finish.1 = (f32[2048,1792]{1,0:T(8,128)}, f32[2048,1792]{1,0:T(8,128)}) custom-call(f32[2048,1792]{1,0:T(8,128)S(1)} %get-tuple-element.4.w_ref, f32[2048,1792]{1,0:T(8,128)S(1)} %get-tuple-element.5.nm_ref), custom_call_target="tpu_custom_call" | custom-call | tf_op jit(solution)/shard_map/finish/pallas_call | solution.py:247

commit v2 on v1

--- a/solution.py
+++ b/solution.py
@@ -11,6 +11,7 @@
 F32 = jnp.float32
 MESH = pl.DeviceIdType.MESH
 MIB = 1 << 20
+TAIL = 32
 
 
 def partner(me, k, n):
@@ -28,11 +29,26 @@
     return lax.rem(me + n - k, n) if n & (n - 1) else partner(me, k, n)
 
 
+def kinds(n):
+    near = [1] if n > 1 else []
+    direct = [k for k in range(2, n) if not (k >> 1) & ((k >> 1) - 1)]
+    return near, direct, [k for k in range(2, n) if k not in direct]
+
+
 def exchange(
-    n, nr, limit, head, step,
-    g_ref, m_ref, w_ref, w_out, nm_out,
+    n, nr, limit, head, step, tail,
+    g_ref, m_ref, w_ref, w_out, nm_out, *refs,
+):
+    near, direct, routed = kinds(n)
+    tail_outs, refs = refs[: len(direct)], refs[len(direct) :]
+    exchange_body(n, nr, limit, head, step, tail, g_ref, m_ref, w_ref, w_out, nm_out, tail_outs, *refs)
+
+
+def exchange_body(
+    n, nr, limit, head, step, tail,
+    g_ref, m_ref, w_ref, w_out, nm_out, tail_outs,
     gbuf, mbuf, part, col_parts, row_parts,
-    g_sem, m_sem, own_sem, w_send, w_recv, nm_send, nm_recv, cs_sem, cr_sem, rs_sem, rr_sem,
+    g_sem, m_sem, own_sem, tail_sem, w_send, w_recv, nm_send, nm_recv, cs_sem, cr_sem, rs_sem, rr_sem,
 ):
     rows, width = g_ref.shape
     cols = width // n
@@ -61,9 +77,7 @@
         return out, arriving
 
     peers = {k: (partner(me, k, n), source(me, k, n)) for k in range(1, n)}
-    near = [k for k in peers if k >> 1 == 0]
-    direct = [k for k in peers if k >> 1 and not (k >> 1) & ((k >> 1) - 1)]
-    routed = [k for k in peers if k not in near and k not in direct]
+    near, direct, routed = kinds(n)
 
     g_loads = [
         pltpu.make_async_copy(g_ref.at[pl.ds(c * step, step)], gbuf.at[pl.ds(c * step, step)], g_sem.at[c])
@@ -83,7 +97,7 @@
     pl.semaphore_wait(barrier, n - 1 + nr - 1)
 
     w_first = {k: piece(w_ref, w_out, *peers[k], 0, head, w_send, w_recv, k, 0) for k in peers}
-    w_rest = {k: piece(w_ref, w_out, *peers[k], head, rows - head, w_send, w_recv, k, 1) for k in peers}
+    w_rest = {k: piece(w_ref, w_out, *peers[k], head, rows - head - (tail if k in direct else 0), w_send, w_recv, k, 1) for k in peers}
     nm_all = {k: piece(gbuf, nm_out, *peers[k], 0, rows, nm_send, nm_recv, k, 0) for k in peers}
 
     for k in direct:
@@ -111,6 +125,10 @@
         m_load(c).start()
     own_w = pltpu.make_async_copy(w_ref.at[:, window(me)], w_out.at[landing(me, 0, rows), :], own_sem.at[0])
     own_w.start()
+    tails = [
+        pltpu.make_async_copy(w_ref.at[pl.ds(rows - tail, tail), window(peers[k][0])], out, tail_sem.at[i])
+        for i, (k, out) in enumerate(zip(direct, tail_outs))
+    ]
 
     def col_share(k, slot):
         return pltpu.make_async_remote_copy(
@@ -171,7 +189,11 @@
         nm_all[k][0].start()
     own_nm = pltpu.make_async_copy(gbuf.at[:, window(me)], nm_out.at[landing(me, 0, rows), :], own_sem.at[1])
     own_nm.start()
-
+    for copy in tails:
+        copy.start()
+
+    for copy in tails:
+        copy.wait()
     for k in peers:
         w_first[k][0].wait_send()
         if k not in routed:
@@ -189,28 +211,55 @@
         nm_all[k][1].wait_recv()
 
 
-def finish(block, w_ref, nm_ref, nw_out, nm_out, buf, nw_sem, nm_sem):
-    rows = w_ref.shape[0]
-    blocks = rows // block
+def finish(n, rows, tail, w_ref, nm_ref, nw_out, nm_out, buf, nw_sem, nm_sem):
+    me = lax.axis_index("col")
+    direct = kinds(n)[1]
     whole = pltpu.make_async_copy(nm_ref, nm_out, nm_sem)
-
-    def write(b):
-        return pltpu.make_async_copy(buf.at[b], nw_out.at[pl.ds(b * block, block)], nw_sem.at[b])
-
-    for b in range(blocks):
-        if b == 1:
-            whole.start()
-
-        def step(r, carry, b=b):
-            start = pl.multiple_of(b * block + r * 8, 8)
-            buf[b, pl.ds(pl.multiple_of(r * 8, 8), 8)] = w_ref[pl.ds(start, 8)] - F32(0.1) * nm_ref[pl.ds(start, 8)]
-            return carry
-
-        lax.fori_loop(0, block // 8, step, 0)
-        write(b).start()
+    whole.start()
+    writes = []
+    for k in range(n):
+        base = (source(me, k, n) if k else me) * rows
+        size = rows - tail if k in direct else rows
+        half = size // 16 * 8
+        for start, count in ((0, half), (half, size - half)):
+
+            def step(r, carry, base=base, start=start, k=k):
+                here = pl.ds(pl.multiple_of(base + start + r * 8, 8), 8)
+                kept = pl.ds(pl.multiple_of(k * rows + start + r * 8, 8), 8)
+                buf[kept] = w_ref[here] - F32(0.1) * nm_ref[here]
+                return carry
+
+            lax.fori_loop(0, count // 8, step, 0)
+            write = pltpu.make_async_copy(
+                buf.at[pl.ds(k * rows + start, count)],
+                nw_out.at[pl.ds(pl.multiple_of(base + start, 8), count)],
+                nw_sem.at[len(writes)],
+            )
+            write.start()
+            writes.append(write)
     whole.wait()
-    for b in range(blocks):
-        write(b).wait()
+    for write in writes:
+        write.wait()
+
+
+def finish_tail(n, rows, tail, *refs):
+    me = lax.axis_index("col")
+    direct = kinds(n)[1]
+    got_refs = refs[1 : 1 + len(direct)]
+    nm_ref, nw_out, got, in_sem, out_sem = refs[1 + len(direct) :]
+    loads = [pltpu.make_async_copy(ref, got.at[i], in_sem.at[i]) for i, ref in enumerate(got_refs)]
+    for load in loads:
+        load.start()
+    writes = []
+    for i, k in enumerate(direct):
+        here = pl.ds(pl.multiple_of(source(me, k, n) * rows + rows - tail, 8), tail)
+        loads[i].wait()
+        got[i] = got[i] - F32(0.1) * nm_ref[here]
+        write = pltpu.make_async_copy(got.at[i], nw_out.at[here], out_sem.at[i])
+        write.start()
+        writes.append(write)
+    for write in writes:
+        write.wait()
 
 
 def body(n, nr, grad, momentum, weight):
@@ -222,18 +271,21 @@
     dma = pltpu.SemaphoreType.DMA
     anywhere, vmem = pl.BlockSpec(memory_space=pl.ANY), pl.BlockSpec(memory_space=pltpu.VMEM)
     local = rows * width * 4
-    w_new, nm_new = pl.pallas_call(
-        functools.partial(exchange, n, nr, limit, head, step),
-        out_shape=(pltpu.VMEM((n * rows, cols), F32),) * 2,
+    tail = min(TAIL, rows // 16 * 8)
+    direct = kinds(n)[1]
+    w_new, nm_new, *tails = pl.pallas_call(
+        functools.partial(exchange, n, nr, limit, head, step, tail),
+        out_shape=(pltpu.VMEM((n * rows, cols), F32),) * 2
+        + (jax.ShapeDtypeStruct((tail, cols), F32),) * len(direct),
         in_specs=[anywhere] * 3,
-        out_specs=(vmem,) * 2,
+        out_specs=(vmem,) * 2 + (anywhere,) * len(direct),
         scratch_shapes=[
             pltpu.VMEM((rows, width), F32),
             pltpu.VMEM((2, step, width), F32),
             pltpu.VMEM((8, 128), F32),
             pltpu.VMEM((n, 8, 128), F32),
             pltpu.VMEM((nr, n, 8, 128), F32),
-            dma((rows // step,)), dma((2,)), dma((2,)),
+            dma((rows // step,)), dma((2,)), dma((2,)), dma((len(direct),)),
             dma((n, 2)), dma((n, 2)), dma((n, 1)), dma((n, 1)),
             dma((n,)), dma((n,)), dma((nr,)), dma((nr,)),
         ],
@@ -243,16 +295,32 @@
         ),
         name="exchange",
     )(grad, momentum, weight)
-    block = n * rows // 16
-    return pl.pallas_call(
-        functools.partial(finish, block),
+    turned = n & (n - 1) == 0
+    got = [
+        lax.ppermute(x, "col", [(d, d ^ k if turned else (d + k) % n) for d in range(n)])
+        for k, x in zip(direct, tails)
+    ]
+    nw, nm = pl.pallas_call(
+        functools.partial(finish, n, rows, tail),
         out_shape=(jax.ShapeDtypeStruct((n * rows, cols), F32),) * 2,
         in_specs=[vmem] * 2,
         out_specs=(anywhere,) * 2,
-        scratch_shapes=[pltpu.VMEM((16, block, cols), F32), dma((16,)), dma],
+        scratch_shapes=[pltpu.VMEM((n * rows, cols), F32), dma((2 * n,)), dma],
         compiler_params=pltpu.CompilerParams(vmem_limit_bytes=local + 2 * MIB),
+        cost_estimate=pl.CostEstimate(flops=2 * rows * width, bytes_accessed=2 * local, transcendentals=0),
         name="finish",
     )(w_new, nm_new)
+    nw = pl.pallas_call(
+        functools.partial(finish_tail, n, rows, tail),
+        out_shape=jax.ShapeDtypeStruct((n * rows, cols), F32),
+        in_specs=[anywhere] * (1 + len(direct)) + [vmem],
+        out_specs=anywhere,
+        scratch_shapes=[pltpu.VMEM((len(direct), tail, cols), F32), dma((len(direct),)), dma((len(direct),))],
+        input_output_aliases={0: 0},
+        compiler_params=pltpu.CompilerParams(vmem_limit_bytes=len(direct) * tail * cols * 4 + 2 * MIB),
+        name="finish_tail",
+    )(nw, *got, nm_new)
+    return nw, nm
 
 
 def solution(mesh):

time: 334 us -> 330 us (0.988)
  Pallas kernels: 333 us -> 325 us
  starting transfers between devices: 0 us -> 3.56 us
    pallas_call x2 -> x3, Pallas kernels: 333 us -> 325 us  [the longest x1 313 us: body(): pl.pallas_call(functools.partial(exchange, n, nr, limit, head, step, tail...]
    ppermute x0 -> x4, starting transfers between devices: none -> 3.56 us  [body(): lax.ppermute(x, 'col', [(d, d ^ k if turned else (d + k) % n) for d in ra...]
  transfers between devices with their start and end apart: 0 -> 4, of which waited for: 0 -> 2; matrix products, arithmetic and copies ran while one was open for 0% -> 0% of each run, Pallas kernels for 0% -> 3%
where the time goes in v2:
time: 330 us; the launch traced here: 329 us
  Pallas kernels  325 us (98%)
  starting transfers between devices  3.56 us (1%)
    pallas_call x1, Pallas kernels, body(): pl.pallas_call(functools.partial(exchange, n, nr, limit, head, step, tail...  313 us
    pallas_call x1, Pallas kernels, body(): pl.pallas_call(functools.partial(finish, n, rows, tail), out_shape=(jax.S...  9.76 us
  transfers between devices with their start and end apart: 4, of which 2 were waited for; matrix products, arithmetic and copies ran while one was open for 0% of the time, Pallas kernels for 3%

profile of v2, /device:TPU:0, one launch (start us, length us, event | category | flops | bytes accessed | tf_op | source)
XLA Modules:
  0.0 329.3 jit_solution(8423135151954195787)
XLA Ops:
  0.6 313.0 %exchange.1 = (f32[2048,1792]{1,0:T(8,128)S(1)}, f32[2048,1792]{1,0:T(8,128)S(1)}, f32[32,1792]{1,0:T(8,128)S(1)}, f32[32,1792]{1,0:T(8,128)S(1)}, f32[32,1792]{1,0:T(8,128)S(1)}, /*index=5*/f32[32,1792]{1,0:T(8,128)S(1)}) custom-call(f32[256,14336]{1,0:T(8,128)} %g_ref.1, f32[256,14336]{1,0:T(8,128)} %m_ref.1, f32[256,14336]{1,0:T(8,128)} %w_ref.1), custom_call_target="tpu_custom_call" | custom-call | tf_op jit(solution)/shard_map/exchange/pallas_call | solution.py:276
  313.7 0.6 collective-permute-start
  314.3 1.8 collective-permute-start.1
  316.0 0.5 collective-permute-start.2
  316.6 0.7 collective-permute-start.3
  317.2 9.8 %finish.1 = (f32[2048,1792]{1,0:T(8,128)}, f32[2048,1792]{1,0:T(8,128)}) custom-call(f32[2048,1792]{1,0:T(8,128)S(1)} %get-tuple-element.10.w_ref, f32[2048,1792]{1,0:T(8,128)S(1)} %get-tuple-element.11.nm_ref.refs_5_), custom_call_target="tpu_custom_call" | custom-call | flops 7340032 | bytes 29360128 | tf_op jit(solution)/shard_map/finish/pallas_call | solution.py:303
  327.0 0.0 collective-permute-done.refs_1_
  327.0 0.1 collective-permute-done.1.refs_2_
  327.1 0.0 collective-permute-done.2.refs_3_
  327.1 0.1 collective-permute-done.3.refs_4_
  327.2 2.2 finish_tail.1
Async XLA Ops:
  313.7 13.3 %collective-permute-start = (f32[32,1792]{1,0:T(8,128)S(1)}, f32[32,1792]{1,0:T(8,128)S(1)}, u32[]{:S(2)}, u32[]{:S(2)}) collective-permute-start(f32[32,1792]{1,0:T(8,128)S(1)} %get-tuple-element.13), channel_id=1, source_target_pairs={{0,2},{1,3},{2,0},{3,1},{4,6},{5,7},{6,4},{7,5},{8,10},{9,11},{10,... | collective-permute-start | bytes 688136 | tf_op jit(solution)/shard_map/ppermute | solution.py:300
  314.3 12.8 %collective-permute-start.1 = (f32[32,1792]{1,0:T(8,128)S(1)}, f32[32,1792]{1,0:T(8,128)S(1)}, u32[]{:S(2)}, u32[]{:S(2)}) collective-permute-start(f32[32,1792]{1,0:T(8,128)S(1)} %get-tuple-element.14), channel_id=1, source_target_pairs={{0,3},{1,2},{2,1},{3,0},{4,7},{5,6},{6,5},{7,4},{8,11},{9,10},{10,... | collective-permute-start | bytes 688136 | tf_op jit(solution)/shard_map/ppermute | solution.py:300
  316.0 11.1 %collective-permute-start.2 = (f32[32,1792]{1,0:T(8,128)S(1)}, f32[32,1792]{1,0:T(8,128)S(1)}, u32[]{:S(2)}, u32[]{:S(2)}) collective-permute-start(f32[32,1792]{1,0:T(8,128)S(1)} %get-tuple-element.15), channel_id=1, source_target_pairs={{0,4},{1,5},{2,6},{3,7},{4,0},{5,1},{6,2},{7,3},{8,12},{9,13},{10,... | collective-permute-start | bytes 688136 | tf_op jit(solution)/shard_map/ppermute | solution.py:300
  316.6 10.6 %collective-permute-start.3 = (f32[32,1792]{1,0:T(8,128)S(1)}, f32[32,1792]{1,0:T(8,128)S(1)}, u32[]{:S(2)}, u32[]{:S(2)}) collective-permute-start(f32[32,1792]{1,0:T(8,128)S(1)} %get-tuple-element.16), channel_id=1, source_target_pairs={{0,5},{1,4},{2,7},{3,6},{4,1},{5,0},{6,3},{7,2},{8,13},{9,12},{10,... | collective-permute-start | bytes 688136 | tf_op jit(solution)/shard_map/ppermute | solution.py:300
